TPU v7x, 32 devices: a whole 2x2x4 slice. The times are simulated.
32 devices in a mesh: grp: 8 (over y, x, core), shard: 4 (over z).
Axes of the slice: x: 2, y: 2, z: 4, core: 2. Of those that a mesh axis runs over, the one named last changes fastest.
Arguments:
- gradients: bfloat16 [8, 1024, 5120], P('grp', None, 'shard'), may hold values from -150 to 150
- left_factor: bfloat16 [8, 1024, 1024], P('grp'), may hold values from -1 to 2, as said below
- right_factor: bfloat16 [8, 5120, 5120], P('grp', 'shard'), may hold values from -1 to 2, as said below
Outputs:
- update: bfloat16 [8, 1024, 5120], P('grp', None, 'shard')
Inputs may be any that keep to these rules, and one draw needn't show every extreme that they name: `left_factor`: each factor is upper triangular with a positive diagonal. `right_factor`: each factor is upper triangular with a positive diagonal.
All inputs are finite; a program needn't handle non-finite values.
Results may differ from a plain program's by a relative error of at most 0.0061.
Values may be sent and summed in bfloat16 or wider, within the bound.
A program may use at most 128 MiB of HBM per device.

v0:
```python
import jax
import jax.numpy as jnp
from jax import lax
from jax.sharding import PartitionSpec as P


def body(gradients, left_factor, right_factor):
    squares = jnp.float32(0.0)
    gradient = gradients[0]
    left_q = left_factor[0]
    right_rows = right_factor[0]
    block = right_rows
    first = lax.dot_general(
        lax.all_gather(gradient, "shard", axis=1, tiled=True),
        block,
        (((1,), (1,)), ((), ())),
        preferred_element_type=jnp.float32,
    ).astype(jnp.bfloat16)
    block = right_rows
    second_rows = lax.psum_scatter(
        lax.dot_general(block, first, (((0,), (1,)), ((), ())), preferred_element_type=jnp.float32),
        "shard",
        scatter_dimension=0,
        tiled=True,
    ).astype(jnp.bfloat16)
    second = second_rows.T
    third = jnp.dot(left_q, second, preferred_element_type=jnp.float32).astype(jnp.bfloat16)
    precond = lax.dot_general(
        left_q, third, (((0,), (0,)), ((), ())), preferred_element_type=jnp.float32
    )
    results = [precond]
    squares = jnp.sum(precond * precond)
    total = lax.psum(squares, ("grp", "shard"))
    count = (
        gradients.shape[0]
        * lax.axis_size("grp")
        * gradients.shape[1]
        * gradients.shape[2]
        * lax.axis_size("shard")
    )
    rms = jnp.sqrt(total / count + 1e-06)
    factor = jnp.minimum(jnp.float32(1.0), 1.1 / rms)
    stacked = jnp.stack(results, axis=0)
    return (stacked * factor).astype(jnp.bfloat16)


def solution(mesh):
    in_specs = (P("grp", None, "shard"), P("grp", None, None), P("grp", "shard", None))
    out_specs = P("grp", None, "shard")
    return jax.shard_map(body, mesh=mesh, in_specs=in_specs, out_specs=out_specs, check_vma=False)
```

profile of v0, /device:TPU:0, one launch (start us, length us, event | category | flops | bytes accessed | tf_op | source)
XLA Modules:
  0.0 647.6 jit_solution(3090217392802980609)
XLA Ops:
  6.5 0.0 copy-start
  6.5 0.0 all-gather.3.cloned.1.call-start
  6.5 0.7 all-gather.3.cloned.1.call-update
  7.3 0.0 reduce-scatter.2.cloned.1.call-start
  7.3 188.3 %all-gather.3.cloned.1.call-done = bf16[1,1024,5120]{2,1,0:T(8,128)(2,1)} async-done(((bf16[1,1024,1280]{2,1,0:T(8,128)(2,1)}), bf16[1,1024,5120]{2,1,0:T(8,128)(2,1)}) %all-gather.3.cloned.1.call-update) | async-done | bytes 10485776 | tf_op jit(solution)/shard_map/all_gather | solution.py:14
  195.6 17.5 %fusion.8 = bf16[1024,1280]{1,0:T(8,128)(2,1)S(1)} fusion(bf16[1,1280,5120]{2,1,0:T(8,128)(2,1)} %param.5, bf16[1,1024,5120]{2,1,0:T(8,128)(2,1)} %all-gather.3.cloned.1.call-done), kind=kOutput, calls=%fused_computation.8 | convolution fusion | flops 13423083520 | bytes 26214400 | tf_op jit(solution)/shard_map/dot_general | solution.py:13
  213.0 20.6 %fusion.4 = f32[5120,1024]{0,1:T(8,128)} fusion(bf16[1024,1280]{1,0:T(8,128)(2,1)S(1)} %fusion.8, bf16[1,1280,5120]{2,1,0:T(8,128)(2,1)} %param.5), kind=kOutput, calls=%fused_computation.4 | convolution fusion | flops 13421772800 | bytes 36700160 | tf_op jit(solution)/shard_map/dot_general | solution.py:21
  233.6 0.0 reduce-scatter.2.cloned.1.call-update
  233.7 345.7 %reduce-scatter.2.cloned.1.call-done = f32[1280,1024]{0,1:T(8,128)} async-done(((f32[5120,1024]{0,1:T(8,128)}), f32[1280,1024]{0,1:T(8,128)}) %reduce-scatter.2.cloned.1.call-update) | async-done | bytes 5242896 | tf_op jit(solution)/shard_map/reduce_scatter | solution.py:20
  579.4 0.0 copy-done
  579.4 9.9 %multiply_reduce_fusion = (f32[]{:T(128)}, f32[1280,1024]{1,0:T(8,128)}) fusion(bf16[1,1024,1024]{2,1,0:T(8,128)(2,1)S(1)} %copy-done, f32[1280,1024]{0,1:T(8,128)} %reduce-scatter.2.cloned.1.call-done), kind=kOutput, calls=%fused_computation.7 | convolution fusion | flops 5373952000 | bytes 12582916 | tf_op jit(solution)/shard_map/dot_general | solution.py:28
  589.3 41.7 %psum.7 = f32[]{:T(128)} all-reduce(f32[]{:T(128)} %get-tuple-element.5), channel_id=1, replica_groups=mesh['grp'=8,'shard'=4] {'grp','shard'}, use_global_device_ids=true, to_apply=%region_2.0 | all-reduce | flops 1 | bytes 8 | tf_op jit(solution)/shard_map/psum | solution.py:33
  631.7 4.7 fusion.13
  636.4 4.4 copy.4
Async XLA Ops:
  6.5 572.8 %copy-start = (bf16[1,1024,1024]{2,1,0:T(8,128)(2,1)S(1)}, bf16[1,1024,1024]{2,1,0:T(8,128)(2,1)}, u32[]{:S(2)}) copy-start(bf16[1,1024,1024]{2,1,0:T(8,128)(2,1)} %param.4) | copy-start | bytes 6291460
  6.5 189.0 %all-gather.3.cloned.1.call-start = ((), (), s32[]{:S(2)}) async-start(), calls=%async_computation.2 | async-start | bytes 13107200 | tf_op jit(solution)/shard_map/all_gather | solution.py:14
  7.3 572.1 %reduce-scatter.2.cloned.1.call-start = ((), (), s32[]{:S(2)}) async-start(), calls=%async_computation.1 | async-start | bytes 26214400 | tf_op jit(solution)/shard_map/reduce_scatter | solution.py:20
Sparse Core Ops, SparseCore 0:
  8.9 186.6 all-gather.2
  233.8 345.5 reduce-scatter.1
where the time goes:
time: 648 us
  waiting for transfers between devices  535 us (83%)
  matrix products  48 us (7%)
  blocking collectives  41.7 us (6%)
  between operations  14.1 us (2%)
    reduce_scatter x1, waiting for transfers between devices, body(): lax.psum_scatter(lax.dot_general(block, first, (((0,), (1,)), ((), ())),...  346 us
    all_gather x1, waiting for transfers between devices, body(): lax.all_gather(gradient, 'shard', axis=1, tiled=True)  188 us
    psum x1, blocking collectives, body(): total = lax.psum(squares, ('grp', 'shard'))  41.7 us
    dot_general x1, matrix products, body(): lax.dot_general(block, first, (((0,), (1,)), ((), ())), preferred_element...  20.6 us
    dot_general x1, matrix products, body(): lax.dot_general(lax.all_gather(gradient, 'shard', axis=1, tiled=True), bl...  17.5 us
  transfers between devices with their start and end apart: 2, of which 2 were waited for; matrix products, arithmetic and copies ran while one was open for 0% of the time, Pallas kernels for 0%

commit v1 on v0

--- a/solution.py
+++ b/solution.py
@@ -30,7 +30,8 @@
     )
     results = [precond]
     squares = jnp.sum(precond * precond)
-    total = lax.psum(squares, ("grp", "shard"))
+    half = lax.psum(squares, "grp")
+    total = lax.psum(half, "shard")
     count = (
         gradients.shape[0]
         * lax.axis_size("grp")

time: 648 us -> 633 us (0.977)
  blocking collectives: 41.7 us -> 26.7 us
    psum x1 -> x2, blocking collectives: 41.7 us -> 26.7 us  [the longest x1 13.8 us: body(): half = lax.psum(squares, 'grp')]
where the time goes in v1:
time: 633 us
  waiting for transfers between devices  535 us (85%)
  matrix products  48 us (8%)
  blocking collectives  26.7 us (4%)
  between operations  14.1 us (2%)
    reduce_scatter x1, waiting for transfers between devices, body(): lax.psum_scatter(lax.dot_general(block, first, (((0,), (1,)), ((), ())),...  346 us
    all_gather x1, waiting for transfers between devices, body(): lax.all_gather(gradient, 'shard', axis=1, tiled=True)  188 us
    dot_general x1, matrix products, body(): lax.dot_general(block, first, (((0,), (1,)), ((), ())), preferred_element...  20.6 us
    dot_general x1, matrix products, body(): lax.dot_general(lax.all_gather(gradient, 'shard', axis=1, tiled=True), bl...  17.5 us
    psum x1, blocking collectives, body(): half = lax.psum(squares, 'grp')  13.8 us
    psum x1, blocking collectives, body(): total = lax.psum(half, 'shard')  12.9 us
  transfers between devices with their start and end apart: 2, of which 2 were waited for; matrix products, arithmetic and copies ran while one was open for 0% of the time, Pallas kernels for 0%

profile of v1, /device:TPU:0, one launch (start us, length us, event | category | flops | bytes accessed | tf_op | source)
XLA Modules:
  0.0 632.7 jit_solution(1848564641300166080)
XLA Ops:
  6.5 0.0 copy-start
  6.5 0.0 all-gather.3.cloned.1.call-start
  6.5 0.7 all-gather.3.cloned.1.call-update
  7.3 0.0 reduce-scatter.2.cloned.1.call-start
  7.3 188.3 %all-gather.3.cloned.1.call-done = bf16[1,1024,5120]{2,1,0:T(8,128)(2,1)} async-done(((bf16[1,1024,1280]{2,1,0:T(8,128)(2,1)}), bf16[1,1024,5120]{2,1,0:T(8,128)(2,1)}) %all-gather.3.cloned.1.call-update) | async-done | bytes 10485776 | tf_op jit(solution)/shard_map/all_gather | solution.py:14
  195.6 17.5 %fusion.8 = bf16[1024,1280]{1,0:T(8,128)(2,1)S(1)} fusion(bf16[1,1280,5120]{2,1,0:T(8,128)(2,1)} %param.5, bf16[1,1024,5120]{2,1,0:T(8,128)(2,1)} %all-gather.3.cloned.1.call-done), kind=kOutput, calls=%fused_computation.8 | convolution fusion | flops 13423083520 | bytes 26214400 | tf_op jit(solution)/shard_map/dot_general | solution.py:13
  213.0 20.6 %fusion.4 = f32[5120,1024]{0,1:T(8,128)} fusion(bf16[1024,1280]{1,0:T(8,128)(2,1)S(1)} %fusion.8, bf16[1,1280,5120]{2,1,0:T(8,128)(2,1)} %param.5), kind=kOutput, calls=%fused_computation.4 | convolution fusion | flops 13421772800 | bytes 36700160 | tf_op jit(solution)/shard_map/dot_general | solution.py:21
  233.6 0.0 reduce-scatter.2.cloned.1.call-update
  233.7 345.7 %reduce-scatter.2.cloned.1.call-done = f32[1280,1024]{0,1:T(8,128)} async-done(((f32[5120,1024]{0,1:T(8,128)}), f32[1280,1024]{0,1:T(8,128)}) %reduce-scatter.2.cloned.1.call-update) | async-done | bytes 5242896 | tf_op jit(solution)/shard_map/reduce_scatter | solution.py:20
  579.4 0.0 copy-done
  579.4 9.9 %multiply_reduce_fusion = (f32[]{:T(128)}, f32[1280,1024]{1,0:T(8,128)}) fusion(bf16[1,1024,1024]{2,1,0:T(8,128)(2,1)S(1)} %copy-done, f32[1280,1024]{0,1:T(8,128)} %reduce-scatter.2.cloned.1.call-done), kind=kOutput, calls=%fused_computation.7 | convolution fusion | flops 5373952000 | bytes 12582916 | tf_op jit(solution)/shard_map/dot_general | solution.py:28
  589.3 13.8 %psum.14 = f32[]{:T(128)} all-reduce(f32[]{:T(128)} %get-tuple-element.5), channel_id=1, replica_groups=mesh['grp'=8,'shard'=4] {'grp'}, use_global_device_ids=true, to_apply=%region_2.0 | all-reduce | flops 1 | bytes 8 | tf_op jit(solution)/shard_map/psum | solution.py:33
  603.1 12.9 %psum.15 = f32[]{:T(128)} all-reduce(f32[]{:T(128)} %psum.14), channel_id=1, replica_groups=mesh['grp'=8,'shard'=4] {'shard'}, use_global_device_ids=true, to_apply=%region_3.0 | all-reduce | flops 1 | bytes 8 | tf_op jit(solution)/shard_map/psum | solution.py:34
  616.7 4.7 fusion.13
  621.5 4.4 copy.4
Async XLA Ops:
  6.5 572.8 %copy-start = (bf16[1,1024,1024]{2,1,0:T(8,128)(2,1)S(1)}, bf16[1,1024,1024]{2,1,0:T(8,128)(2,1)}, u32[]{:S(2)}) copy-start(bf16[1,1024,1024]{2,1,0:T(8,128)(2,1)} %param.4) | copy-start | bytes 6291460
  6.5 189.0 %all-gather.3.cloned.1.call-start = ((), (), s32[]{:S(2)}) async-start(), calls=%async_computation.2 | async-start | bytes 13107200 | tf_op jit(solution)/shard_map/all_gather | solution.py:14
  7.3 572.1 %reduce-scatter.2.cloned.1.call-start = ((), (), s32[]{:S(2)}) async-start(), calls=%async_computation.1 | async-start | bytes 26214400 | tf_op jit(solution)/shard_map/reduce_scatter | solution.py:20
Sparse Core Ops, SparseCore 0:
  8.9 186.6 all-gather.2
  233.8 345.5 reduce-scatter.1
